TPU v7x, 32 devices: a whole 2x2x4 slice. The times are simulated.
32 devices in a mesh: nest: 4 (over x, core), py: 2 (over y), px: 4 (over z).
Axes of the slice: x: 2, y: 2, z: 4, core: 2. Of those that a mesh axis runs over, the one named last changes fastest.
Arguments:
- initial_state: float32 [4, 4, 256, 256], P('nest', None, 'px', 'py'), may hold values from -6 to 6
- drive_modes: float32 [3, 4, 64, 64], replicated, may hold values from -6 to 6
- relax_rates: float32 [4, 4], P('nest'), may hold values from 0.2 to 0.9
- nest_offsets: int32 [4, 2], replicated, may hold values from 0 to 170
Outputs:
- final_state: float32 [4, 4, 256, 256], P('nest', None, 'px', 'py')
- final_modes: float32 [4, 4, 64, 64], P('nest')
Inputs may be any that keep to these rules, and one draw needn't show every extreme that they name: `nest_offsets`: row 0 is not read.
All inputs are finite; a program needn't handle non-finite values.
Results may differ from a plain program's by a relative error of at most 0.0001.
Values sent between devices are 32-bit elements; how exact they have to be, the bound alone decides.
A program may use at most 64 MiB of HBM per device.

v0:
```python
import math
import jax
import jax.numpy as jnp
import numpy as np
from jax import lax
from jax.sharding import PartitionSpec as P

RATIO = 3
RATE = 0.2
HI = lax.Precision.HIGH


def basis(cells, modes, refine, fn=np.cos):
    j = np.arange(modes, dtype=np.int64)
    q = 2 * np.arange(cells, dtype=np.int64) + 1
    product = j[None, :] * q[:, None] % (4 * refine * cells)
    weight = np.where(j == 0, 1.0, 2.0) / cells
    return np.sqrt(weight)[None, :] * fn(np.pi * product / (2.0 * refine * cells))


def half_step(table):
    pad = np.pad(table, ((1, 1), (0, 0)))
    return (0.5 - 2 * RATE) * table + RATE * (pad[2:] + pad[:-2])


def powers(table, count):
    out = [table]
    for _ in range(count):
        out.append(half_step(out[-1]))
    return out


def offset_map(cells, modes, offset):
    base = basis(cells, modes, 1)
    even = jnp.asarray(base.T @ basis(cells, modes, RATIO), jnp.float32)
    odd = jnp.asarray(base.T @ basis(cells, modes, RATIO, np.sin), jnp.float32)
    j = jnp.arange(modes, dtype=jnp.int32)
    product = j * (2 * RATIO * offset) % (4 * RATIO * cells)
    angle = jnp.pi * product.astype(jnp.float32) / (2.0 * RATIO * cells)
    return even * jnp.cos(angle)[None, :] - odd * jnp.sin(angle)[None, :]


def exchange(value, axis, dim, width):
    n, length = (lax.axis_size(axis), value.shape[dim])
    up = [(i, i + 1) for i in range(n - 1)]
    down = [(i + 1, i) for i in range(n - 1)]
    before = lax.ppermute(lax.slice_in_dim(value, length - width, length, axis=dim), axis, up)
    after = lax.ppermute(lax.slice_in_dim(value, 0, width, axis=dim), axis, down)
    return jnp.concatenate([before, value, after], axis=dim)


def free_steps(field, total_x, total_y, steps):
    levels, cx, cy = field.shape
    pad = exchange(exchange(field, "py", 2, steps), "px", 1, steps)
    gx = lax.axis_index("px") * cx - steps + jnp.arange(cx + 2 * steps)
    gy = lax.axis_index("py") * cy - steps + jnp.arange(cy + 2 * steps)
    inside = ((gx >= 0) & (gx < total_x))[:, None] & ((gy >= 0) & (gy < total_y))[None, :]
    for s in range(steps):
        mid = pad[:, 1:-1, 1:-1]
        near = pad[:, 2:, 1:-1] + pad[:, :-2, 1:-1] + pad[:, 1:-1, 2:] + pad[:, 1:-1, :-2]
        pad = mid + RATE * (near - 4.0 * mid)
        cut = s + 1
        pad = jnp.where(inside[cut:-cut, cut:-cut][None], pad, 0.0)
    return pad


def body(initial_state, drive_modes, relax_rates, nest_offsets):
    k = lax.axis_index("nest")
    nests = lax.axis_size("nest")
    field = initial_state[0]
    levels, cx, cy = field.shape
    windows, _, m, _ = drive_modes.shape
    nx, ny = (cx * lax.axis_size("px"), cy * lax.axis_size("py"))
    rp, cp = (powers(basis(nx, m, 1), windows), powers(basis(ny, m, 1), windows))
    a = [jnp.asarray(rp[0].T @ t, jnp.float32) for t in rp]
    b = [jnp.asarray(cp[0].T @ t, jnp.float32) for t in cp]
    u_all = jnp.asarray(np.concatenate(rp, 1), jnp.float32)
    v_all = jnp.asarray(np.concatenate(cp, 1), jnp.float32)
    u = lax.dynamic_slice_in_dim(u_all, lax.axis_index("px") * cx, cx, 0)
    v = lax.dynamic_slice_in_dim(v_all, lax.axis_index("py") * cy, cy, 0)
    half = jnp.einsum("lxy,yq->lxq", field, v, precision=HI)
    rows = []
    for w in range(1, windows + 1):
        terms = [math.comb(w, i) * half[:, :, (w - i) * m : (w - i + 1) * m] for i in range(w + 1)]
        rows.append(
            jnp.einsum(
                "xj,lxm->ljm",
                jnp.concatenate([u[:, i * m : (i + 1) * m] for i in range(w + 1)], 0),
                jnp.concatenate(terms, 1),
                precision=HI,
            )
        )
    shares = lax.psum(jnp.stack(rows), ("py", "px"))
    gain = relax_rates[0][:, None, None]
    row_map = offset_map(nx, m, nest_offsets[k, 0])
    col_map = offset_map(ny, m, nest_offsets[k, 1])

    def left(t, x):
        return jnp.einsum("jp,lpq->ljq", t, x, precision=HI)

    def right(x, t):
        return jnp.einsum("ljq,mq->ljm", x, t, precision=HI)

    def spread(d, x):
        out = left(a[d], x) + right(x, b[d])
        for i in range(1, d):
            out = out + math.comb(d, i) * right(left(a[i], x), b[d - i])
        return out

    parent = jnp.zeros_like(drive_modes)
    for stage in range(nests):
        if stage:
            parent = lax.ppermute(coeffs, "nest", [(i, i + 1) for i in range(nests - 1)])
            interp = jnp.einsum("jp,wlpq->wljq", row_map, parent, precision=HI)
            interp = jnp.einsum("wljq,mq->wljm", interp, col_map, precision=HI)
            target = jnp.where(k == 0, drive_modes, interp)
        else:
            target = drive_modes
        changes, kept = ([], [])
        for w in range(windows):
            own = shares[w]
            for e in range(w):
                own = own + spread(w - e, changes[e])
            changes.append(gain * (target[w] - own))
            kept.append(own + changes[-1])
        coeffs = jnp.stack(kept)
    free = free_steps(field, nx, ny, windows)
    zero = jnp.zeros_like(changes[0])
    blocks = [
        jnp.concatenate(
            [
                math.comb(i + j, i) * changes[windows - 1 - i - j] if i + j < windows else zero
                for j in range(windows)
            ],
            2,
        )
        for i in range(windows)
    ]
    mixed = jnp.concatenate(blocks, 1)
    wide = windows * m
    back = jnp.einsum("lpq,yq->lpy", mixed, v[:, :wide], precision=HI)
    final = free + jnp.einsum("xp,lpy->lxy", u[:, :wide], back, precision=HI)
    return (final[None], coeffs[windows - 1][None])


def solution(mesh):
    spec = P("nest", None, "px", "py")
    return jax.shard_map(
        body,
        mesh=mesh,
        in_specs=(spec, P(), P("nest", None), P()),
        out_specs=(spec, P("nest", None, None, None)),
        check_vma=False,
    )
```

profile of v0, /device:TPU:1, one launch (start us, length us, event | category | flops | bytes accessed | tf_op | source)
XLA Modules:
  0.0 132.8 jit_solution(5296330586854888723)
XLA Ops:
  7.2 1.2 convolution_bitcast_fusion.3
  8.6 0.8 copy-done.7
  9.5 0.3 convolution_bitcast_fusion.19
  9.8 0.3 convolution_bitcast_fusion.6
  10.1 0.3 convolution_bitcast_fusion.5
  10.4 0.8 pad_maximum_fusion
  11.2 0.9 copy-done.3
  12.2 4.1 %collective-permute-start = (f32[4,64,3]{2,1,0:T(8,128)S(1)}, f32[4,64,3]{2,1,0:T(8,128)S(1)}, u32[]{:S(2)}, u32[]{:S(2)}) collective-permute-start(f32[4,64,3]{2,1,0:T(8,128)S(1)} %get-tuple-element.23), channel_id=1, source_target_pairs={{0,4},{1,5},{2,6},{3,7},{8,12},{9,13},{10,14},{11,15},{16,20},{17,... | collective-permute-start | bytes 9224 | tf_op jit(solution)/shard_map/ppermute | solution.py:47
  16.3 1.3 collective-permute-start.1
  17.6 0.7 copy-done.9
  18.3 0.6 constant_dynamic-slice_fusion.2
  20.3 4.1 %collective-permute-done.1 = f32[4,64,3]{2,1,0:T(8,128)S(1)} collective-permute-done((f32[4,64,3]{2,1,0:T(8,128)S(1)}, f32[4,64,3]{2,1,0:T(8,128)S(1)}, u32[]{:S(2)}, u32[]{:S(2)}) %collective-permute-start.1) | collective-permute-done | bytes 3104 | tf_op jit(solution)/shard_map/ppermute | solution.py:48
  24.6 3.2 %collective-permute-start.2 = (f32[4,3,134]{2,1,0:T(4,128)S(1)}, f32[4,3,134]{2,1,0:T(4,128)S(1)}, u32[]{:S(2)}, u32[]{:S(2)}) collective-permute-start(f32[4,3,134]{2,1,0:T(4,128)S(1)} %get-tuple-element.10), channel_id=1, source_target_pairs={{0,1},{1,2},{2,3},{4,5},{5,6},{6,7},{8,9},{9,10},{10,11},{12,13},{... | collective-permute-start | bytes 19304 | tf_op jit(solution)/shard_map/ppermute | solution.py:47
  27.8 1.3 collective-permute-start.3
  29.1 54.7 %all-reduce.3.cloned.1.call-done = f32[3,4,64,64]{3,2,1,0:T(8,128)} async-done(((f32[3,4,64,64]{3,2,1,0:T(8,128)}), f32[3,4,64,64]{3,2,1,0:T(8,128)}) %all-reduce.3.cloned.1.call-update) | async-done | bytes 196624 | tf_op jit(solution)/shard_map/psum | solution.py:93
  83.8 1.0 bitcast_multiply_fusion.2
  85.2 0.6 copy-done.2
  86.0 0.3 convolution_bitcast_fusion.16
  86.4 0.3 convolution_add_fusion.9
  86.7 0.5 copy-done.4
  87.7 5.6 %collective-permute-start.4 = (f32[3,4,64,64]{3,2,1,0:T(8,128)S(1)}, f32[3,4,64,64]{3,2,1,0:T(8,128)S(1)}, u32[]{:S(2)}, u32[]{:S(2)}) collective-permute-start(f32[3,4,64,64]{3,2,1,0:T(8,128)S(1)} %pad_maximum_fusion.1), channel_id=1, source_target_pairs={{0,8},{8,16},{16,24},{1,9},{9,17},{17,25},{2,10},{10,18},{18,26},{... | collective-permute-start | bytes 589832 | tf_op jit(solution)/shard_map/ppermute | solution.py:113
  94.0 4.1 %collective-permute-done.4 = f32[3,4,64,64]{3,2,1,0:T(8,128)S(1)} collective-permute-done((f32[3,4,64,64]{3,2,1,0:T(8,128)S(1)}, f32[3,4,64,64]{3,2,1,0:T(8,128)S(1)}, u32[]{:S(2)}, u32[]{:S(2)}) %collective-permute-start.4) | collective-permute-done | bytes 196640 | tf_op jit(solution)/shard_map/ppermute | solution.py:113
  98.0 0.3 convolution_bitcast_fusion.2
  98.4 0.3 convolution_select_fusion.2
  98.8 0.3 convolution_bitcast_fusion.15
  99.0 0.3 fusion.6
  99.4 0.3 convolution_bitcast_fusion.13
  99.9 0.3 convolution_bitcast_fusion.14
  100.4 0.3 fusion.71
  100.7 4.4 %collective-permute-start.5 = (f32[3,4,64,64]{3,2,1,0:T(8,128)S(1)}, f32[3,4,64,64]{3,2,1,0:T(8,128)S(1)}, u32[]{:S(2)}, u32[]{:S(2)}) collective-permute-start(f32[3,4,64,64]{3,2,1,0:T(8,128)S(1)} %pad_maximum_fusion.2), channel_id=1, source_target_pairs={{0,8},{8,16},{16,24},{1,9},{9,17},{17,25},{2,10},{10,18},{18,26},{... | collective-permute-start | bytes 589832 | tf_op jit(solution)/shard_map/ppermute | solution.py:113
  105.1 0.4 fusion.54
  105.5 4.3 %collective-permute-done.5 = f32[3,4,64,64]{3,2,1,0:T(8,128)S(1)} collective-permute-done((f32[3,4,64,64]{3,2,1,0:T(8,128)S(1)}, f32[3,4,64,64]{3,2,1,0:T(8,128)S(1)}, u32[]{:S(2)}, u32[]{:S(2)}) %collective-permute-start.5) | collective-permute-done | bytes 196640 | tf_op jit(solution)/shard_map/ppermute | solution.py:113
  109.8 0.3 convolution_bitcast_fusion.1
  110.2 0.3 convolution_select_fusion.1
  110.6 0.3 convolution_bitcast_fusion.12
  110.8 0.3 fusion.10
  111.2 0.3 convolution_bitcast_fusion.10
  111.7 0.3 convolution_bitcast_fusion.11
  112.0 0.3 convolution_add_fusion.3
  112.2 0.3 fusion.65
  112.6 4.4 %collective-permute-start.6 = (f32[3,4,64,64]{3,2,1,0:T(8,128)S(1)}, f32[3,4,64,64]{3,2,1,0:T(8,128)S(1)}, u32[]{:S(2)}, u32[]{:S(2)}) collective-permute-start(f32[3,4,64,64]{3,2,1,0:T(8,128)S(1)} %pad_maximum_fusion.3), channel_id=1, source_target_pairs={{0,8},{8,16},{16,24},{1,9},{9,17},{17,25},{2,10},{10,18},{18,26},{... | collective-permute-start | bytes 589832 | tf_op jit(solution)/shard_map/ppermute | solution.py:113
  117.0 0.4 fusion.50
  117.3 4.3 %collective-permute-done.6 = f32[3,4,64,64]{3,2,1,0:T(8,128)S(1)} collective-permute-done((f32[3,4,64,64]{3,2,1,0:T(8,128)S(1)}, f32[3,4,64,64]{3,2,1,0:T(8,128)S(1)}, u32[]{:S(2)}, u32[]{:S(2)}) %collective-permute-start.6) | collective-permute-done | bytes 196640 | tf_op jit(solution)/shard_map/ppermute | solution.py:113
  121.7 0.3 convolution_bitcast_fusion
  122.0 0.3 convolution_select_fusion
  123.6 0.9 add_bitcast_fusion
  124.5 0.5 fusion.20
  125.1 0.9 fusion.1
  (59 shorter events, 4.8 us)
Async XLA Ops:
  7.2 76.6 %all-reduce.3.cloned.1.call-start = ((), (), s32[]{:S(2)}) async-start(), calls=%async_computation | async-start | bytes 786432 | tf_op jit(solution)/shard_map/psum | solution.py:93
  8.4 1.0 copy-start.7
  11.2 0.9 copy-start.3
  12.1 71.7 %copy-start.1 = (f32[3,4,64,64]{3,2,1,0:T(8,128)S(1)}, f32[3,4,64,64]{3,2,1,0:T(8,128)}, u32[]{:S(2)}) copy-start(f32[3,4,64,64]{3,2,1,0:T(8,128)} %param.15) | copy-start | bytes 589828
  12.2 8.2 %collective-permute-start = (f32[4,64,3]{2,1,0:T(8,128)S(1)}, f32[4,64,3]{2,1,0:T(8,128)S(1)}, u32[]{:S(2)}, u32[]{:S(2)}) collective-permute-start(f32[4,64,3]{2,1,0:T(8,128)S(1)} %get-tuple-element.23), channel_id=1, source_target_pairs={{0,4},{1,5},{2,6},{3,7},{8,12},{9,13},{10,14},{11,15},{16,20},{17,... | collective-permute-start | bytes 9224 | tf_op jit(solution)/shard_map/ppermute | solution.py:47
  16.3 8.2 %collective-permute-start.1 = (f32[4,64,3]{2,1,0:T(8,128)S(1)}, f32[4,64,3]{2,1,0:T(8,128)S(1)}, u32[]{:S(2)}, u32[]{:S(2)}) collective-permute-start(f32[4,64,3]{2,1,0:T(8,128)S(1)} %get-tuple-element.24), channel_id=1, source_target_pairs={{4,0},{5,1},{6,2},{7,3},{12,8},{13,9},{14,10},{15,11},{20,16},{21,... | collective-permute-start | bytes 9224 | tf_op jit(solution)/shard_map/ppermute | solution.py:48
  17.6 0.7 copy-start.9
  24.6 69.2 %collective-permute-start.2 = (f32[4,3,134]{2,1,0:T(4,128)S(1)}, f32[4,3,134]{2,1,0:T(4,128)S(1)}, u32[]{:S(2)}, u32[]{:S(2)}) collective-permute-start(f32[4,3,134]{2,1,0:T(4,128)S(1)} %get-tuple-element.10), channel_id=1, source_target_pairs={{0,1},{1,2},{2,3},{4,5},{5,6},{6,7},{8,9},{9,10},{10,11},{12,13},{... | collective-permute-start | bytes 19304 | tf_op jit(solution)/shard_map/ppermute | solution.py:47
  27.8 56.0 %copy-start.8 = (f32[1,4]{1,0:T(1,128)S(1)}, f32[1,4]{1,0:T(1,128)}, u32[]{:S(2)}) copy-start(f32[1,4]{1,0:T(1,128)} %param.16) | copy-start | bytes 52
  27.8 65.9 %collective-permute-start.3 = (f32[4,3,134]{2,1,0:T(4,128)S(1)}, f32[4,3,134]{2,1,0:T(4,128)S(1)}, u32[]{:S(2)}, u32[]{:S(2)}) collective-permute-start(f32[4,3,134]{2,1,0:T(4,128)S(1)} %get-tuple-element.11), channel_id=1, source_target_pairs={{1,0},{2,1},{3,2},{5,4},{6,5},{7,6},{9,8},{10,9},{11,10},{13,12},{... | collective-permute-start | bytes 19304 | tf_op jit(solution)/shard_map/ppermute | solution.py:48
  83.8 1.0 copy-start
  84.8 1.0 copy-start.2
  86.4 0.8 copy-start.4
  87.7 10.3 %collective-permute-start.4 = (f32[3,4,64,64]{3,2,1,0:T(8,128)S(1)}, f32[3,4,64,64]{3,2,1,0:T(8,128)S(1)}, u32[]{:S(2)}, u32[]{:S(2)}) collective-permute-start(f32[3,4,64,64]{3,2,1,0:T(8,128)S(1)} %pad_maximum_fusion.1), channel_id=1, source_target_pairs={{0,8},{8,16},{16,24},{1,9},{9,17},{17,25},{2,10},{10,18},{18,26},{... | collective-permute-start | bytes 589832 | tf_op jit(solution)/shard_map/ppermute | solution.py:113
  93.7 4.3 %copy-start.5 = (f32[64,64]{1,0:T(8,128)S(1)}, f32[64,64]{1,0:T(8,128)}, u32[]{:S(2)}) copy-start(f32[64,64]{1,0:T(8,128)} %constant.86.clone) | copy-start | bytes 49156
  93.7 4.3 %copy-start.6 = (f32[64,64]{1,0:T(8,128)S(1)}, f32[64,64]{1,0:T(8,128)}, u32[]{:S(2)}) copy-start(f32[64,64]{1,0:T(8,128)} %constant.87.clone) | copy-start | bytes 49156
  100.7 9.1 %collective-permute-start.5 = (f32[3,4,64,64]{3,2,1,0:T(8,128)S(1)}, f32[3,4,64,64]{3,2,1,0:T(8,128)S(1)}, u32[]{:S(2)}, u32[]{:S(2)}) collective-permute-start(f32[3,4,64,64]{3,2,1,0:T(8,128)S(1)} %pad_maximum_fusion.2), channel_id=1, source_target_pairs={{0,8},{8,16},{16,24},{1,9},{9,17},{17,25},{2,10},{10,18},{18,26},{... | collective-permute-start | bytes 589832 | tf_op jit(solution)/shard_map/ppermute | solution.py:113
  112.6 9.1 %collective-permute-start.6 = (f32[3,4,64,64]{3,2,1,0:T(8,128)S(1)}, f32[3,4,64,64]{3,2,1,0:T(8,128)S(1)}, u32[]{:S(2)}, u32[]{:S(2)}) collective-permute-start(f32[3,4,64,64]{3,2,1,0:T(8,128)S(1)} %pad_maximum_fusion.3), channel_id=1, source_target_pairs={{0,8},{8,16},{16,24},{1,9},{9,17},{17,25},{2,10},{10,18},{18,26},{... | collective-permute-start | bytes 589832 | tf_op jit(solution)/shard_map/ppermute | solution.py:113
Sparse Core Ops, SparseCore 0:
  11.3 72.4 all-reduce.2
where the time goes:
time: 133 us
  waiting for transfers between devices  71.5 us (54%)
  starting transfers between devices  24.4 us (18%)
  between operations  16 us (12%)
  matrix products  12.6 us (9%)
  local copies, waits for them, and re-layouts  4.49 us (3%)
  other arithmetic  3.84 us (3%)
    psum x1, waiting for transfers between devices, body(): shares = lax.psum(jnp.stack(rows), ('py', 'px'))  54.7 us
    ppermute x3, starting transfers between devices, body(): lax.ppermute(coeffs, 'nest', [(i, i + 1) for i in range(nests - 1)])  14.4 us
    ppermute x3, waiting for transfers between devices, body(): lax.ppermute(coeffs, 'nest', [(i, i + 1) for i in range(nests - 1)])  12.7 us
    ppermute x2, starting transfers between devices, exchange(): lax.ppermute(lax.slice_in_dim(value, length - width, length, axis=dim), a...  7.35 us
    dot_general x16, matrix products, right(): return jnp.einsum('ljq,mq->ljm', x, t, precision=HI)  4.38 us
    ppermute x2, waiting for transfers between devices, exchange(): lax.ppermute(lax.slice_in_dim(value, 0, width, axis=dim), axis, down)  4.13 us
    unnamed x20, local copies, waits for them, and re-layouts  3.45 us
    dot_general x12, matrix products, left(): return jnp.einsum('jp,lpq->ljq', t, x, precision=HI)  2.86 us
  transfers between devices with their start and end apart: 8, of which 5 were waited for; matrix products, arithmetic and copies ran while one was open for 4% of the time, Pallas kernels for 0%

commit v1 on v0

--- a/solution.py
+++ b/solution.py
@@ -90,7 +90,7 @@
                 precision=HI,
             )
         )
-    shares = lax.psum(jnp.stack(rows), ("py", "px"))
+    shares = jnp.sum(lax.all_gather(jnp.stack(rows), ("py", "px")), axis=0)
     gain = relax_rates[0][:, None, None]
     row_map = offset_map(nx, m, nest_offsets[k, 0])
     col_map = offset_map(ny, m, nest_offsets[k, 1])

time: 133 us -> 123 us (0.925)
  waiting for transfers between devices: 71.5 us -> 61.8 us
  local copies, waits for them, and re-layouts: 4.49 us -> 2.88 us
    psum x1 -> x0, waiting for transfers between devices: 54.7 us -> none  [body(): shares = lax.psum(jnp.stack(rows), ('py', 'px'))]
    all_gather x0 -> x1, waiting for transfers between devices: none -> 46.7 us  [body(): shares = jnp.sum(lax.all_gather(jnp.stack(rows), ('py', 'px')), axis=0)]
    unnamed x20 -> x18, local copies, waits for them, and re-layouts: 3.45 us -> 0.05 us
    reduce_sum x0 -> x1, other arithmetic: none -> 2.28 us  [body(): shares = jnp.sum(lax.all_gather(jnp.stack(rows), ('py', 'px')), axis=0)]
    ppermute x2, waiting for transfers between devices: 4.13 us -> 2.31 us  [exchange(): lax.ppermute(lax.slice_in_dim(value, 0, width, axis=dim), axis, down)]
  transfers between devices with their start and end apart: 8 -> 8, of which waited for: 5 -> 5; matrix products, arithmetic and copies ran while one was open for 4% -> 5% of each run, Pallas kernels for 0% -> 0%
where the time goes in v1:
time: 123 us; the launch traced here: 122 us
  waiting for transfers between devices  61.8 us (50%)
  starting transfers between devices  24 us (20%)
  between operations  16 us (13%)
  matrix products  13.3 us (11%)
  other arithmetic  4.44 us (4%)
  local copies, waits for them, and re-layouts  2.88 us (2%)
    all_gather x1, waiting for transfers between devices, body(): shares = jnp.sum(lax.all_gather(jnp.stack(rows), ('py', 'px')), axis=0)  46.7 us
    ppermute x3, starting transfers between devices, body(): lax.ppermute(coeffs, 'nest', [(i, i + 1) for i in range(nests - 1)])  14.2 us
    ppermute x3, waiting for transfers between devices, body(): lax.ppermute(coeffs, 'nest', [(i, i + 1) for i in range(nests - 1)])  12.7 us
    ppermute x2, starting transfers between devices, exchange(): lax.ppermute(lax.slice_in_dim(value, length - width, length, axis=dim), a...  7.15 us
    dot_general x16, matrix products, right(): return jnp.einsum('ljq,mq->ljm', x, t, precision=HI)  4.38 us
    dot_general x12, matrix products, left(): return jnp.einsum('jp,lpq->ljq', t, x, precision=HI)  2.86 us
    ppermute x2, starting transfers between devices, exchange(): lax.ppermute(lax.slice_in_dim(value, 0, width, axis=dim), axis, down)  2.58 us
  transfers between devices with their start and end apart: 8, of which 5 were waited for; matrix products, arithmetic and copies ran while one was open for 5% of the time, Pallas kernels for 0%

profile of v1, /device:TPU:1, one launch (start us, length us, event | category | flops | bytes accessed | tf_op | source)
XLA Modules:
  0.0 122.4 jit_solution(1179527973240210395)
XLA Ops:
  7.2 1.3 %convolution_bitcast_fusion.3 = f32[4,64,256]{2,1,0:T(8,128)S(1)} fusion(f32[256,256]{1,0:T(8,128)} %constant.85.clone, s32[]{:T(128)S(6)} %select_n.67, f32[1,4,64,128]{3,2,1,0:T(8,128)} %param.14), kind=kOutput, calls=%fused_computation.6 | convolution fusion | flops 50331648 | bytes 524292 | tf_op jit(solution)/shard_map/lxy,yq->lxq/dot_general | solution.py:81
  8.6 1.0 constant_dynamic-slice_fusion
  9.6 0.4 convolution_bitcast_fusion.19
  10.0 0.5 convolution_bitcast_fusion.6
  10.5 0.6 convolution_bitcast_fusion.5
  11.2 0.9 copy.46
  12.2 4.0 %collective-permute-start = (f32[4,64,3]{2,1,0:T(8,128)S(1)}, f32[4,64,3]{2,1,0:T(8,128)S(1)}, u32[]{:S(2)}, u32[]{:S(2)}) collective-permute-start(f32[4,64,3]{2,1,0:T(8,128)S(1)} %get-tuple-element.23), channel_id=1, source_target_pairs={{0,4},{1,5},{2,6},{3,7},{8,12},{9,13},{10,14},{11,15},{16,20},{17,... | collective-permute-start | bytes 9224 | tf_op jit(solution)/shard_map/ppermute | solution.py:47
  16.2 1.3 %collective-permute-start.1 = (f32[4,64,3]{2,1,0:T(8,128)S(1)}, f32[4,64,3]{2,1,0:T(8,128)S(1)}, u32[]{:S(2)}, u32[]{:S(2)}) collective-permute-start(f32[4,64,3]{2,1,0:T(8,128)S(1)} %get-tuple-element.24), channel_id=1, source_target_pairs={{4,0},{5,1},{6,2},{7,3},{12,8},{13,9},{14,10},{15,11},{20,16},{21,... | collective-permute-start | bytes 9224 | tf_op jit(solution)/shard_map/ppermute | solution.py:48
  17.5 0.6 constant_dynamic-slice_fusion.2
  19.6 2.3 %collective-permute-done.1 = f32[4,64,3]{2,1,0:T(8,128)S(1)} collective-permute-done((f32[4,64,3]{2,1,0:T(8,128)S(1)}, f32[4,64,3]{2,1,0:T(8,128)S(1)}, u32[]{:S(2)}, u32[]{:S(2)}) %collective-permute-start.1) | collective-permute-done | bytes 3104 | tf_op jit(solution)/shard_map/ppermute | solution.py:48
  22.0 3.2 %collective-permute-start.2 = (f32[4,3,134]{2,1,0:T(4,128)S(1)}, f32[4,3,134]{2,1,0:T(4,128)S(1)}, u32[]{:S(2)}, u32[]{:S(2)}) collective-permute-start(f32[4,3,134]{2,1,0:T(4,128)S(1)} %get-tuple-element.10), channel_id=1, source_target_pairs={{0,1},{1,2},{2,3},{4,5},{5,6},{6,7},{8,9},{9,10},{10,11},{12,13},{... | collective-permute-start | bytes 19304 | tf_op jit(solution)/shard_map/ppermute | solution.py:47
  25.2 1.3 %collective-permute-start.3 = (f32[4,3,134]{2,1,0:T(4,128)S(1)}, f32[4,3,134]{2,1,0:T(4,128)S(1)}, u32[]{:S(2)}, u32[]{:S(2)}) collective-permute-start(f32[4,3,134]{2,1,0:T(4,128)S(1)} %get-tuple-element.11), channel_id=1, source_target_pairs={{1,0},{2,1},{3,2},{5,4},{6,5},{7,6},{9,8},{10,9},{11,10},{13,12},{... | collective-permute-start | bytes 19304 | tf_op jit(solution)/shard_map/ppermute | solution.py:48
  26.5 46.7 %all-gather.3.cloned.1.call-done = f32[24,4,64,64]{3,2,1,0:T(8,128)} async-done(((f32[3,4,64,64]{3,2,1,0:T(8,128)}), f32[24,4,64,64]{3,2,1,0:T(8,128)}) %all-gather.3.cloned.1.call-update) | async-done | bytes 1572880 | tf_op jit(solution)/shard_map/all_gather | solution.py:93
  73.2 2.3 %reduce_sum.9 = f32[3,4,64,64]{3,2,1,0:T(8,128)S(1)} reduce(f32[8,3,4,64,64]{4,3,2,1,0:T(8,128)} %bitcast.271, f32[]{:T(128)} %constant.37.clone.1), dimensions={0}, to_apply=%region_0.0 | reduce | flops 344064 | bytes 1769476 | tf_op jit(solution)/shard_map/reduce_sum | solution.py:93
  75.8 0.2 fusion.2
  76.3 0.3 convolution_bitcast_fusion.16
  76.7 0.3 convolution_add_fusion.9
  77.2 0.2 fusion.86
  77.5 5.4 %collective-permute-start.4 = (f32[3,4,64,64]{3,2,1,0:T(8,128)S(1)}, f32[3,4,64,64]{3,2,1,0:T(8,128)S(1)}, u32[]{:S(2)}, u32[]{:S(2)}) collective-permute-start(f32[3,4,64,64]{3,2,1,0:T(8,128)S(1)} %pad_maximum_fusion.1), channel_id=1, source_target_pairs={{0,8},{8,16},{16,24},{1,9},{9,17},{17,25},{2,10},{10,18},{18,26},{... | collective-permute-start | bytes 589832 | tf_op jit(solution)/shard_map/ppermute | solution.py:113
  83.5 4.1 %collective-permute-done.4 = f32[3,4,64,64]{3,2,1,0:T(8,128)S(1)} collective-permute-done((f32[3,4,64,64]{3,2,1,0:T(8,128)S(1)}, f32[3,4,64,64]{3,2,1,0:T(8,128)S(1)}, u32[]{:S(2)}, u32[]{:S(2)}) %collective-permute-start.4) | collective-permute-done | bytes 196640 | tf_op jit(solution)/shard_map/ppermute | solution.py:113
  87.6 0.3 convolution_bitcast_fusion.2
  87.9 0.3 convolution_select_fusion.2
  88.3 0.3 convolution_bitcast_fusion.15
  88.6 0.3 fusion.6
  88.9 0.3 convolution_bitcast_fusion.13
  89.4 0.3 convolution_bitcast_fusion.14
  89.7 0.3 convolution_add_fusion.6
  90.0 0.3 fusion.71
  90.3 4.4 %collective-permute-start.5 = (f32[3,4,64,64]{3,2,1,0:T(8,128)S(1)}, f32[3,4,64,64]{3,2,1,0:T(8,128)S(1)}, u32[]{:S(2)}, u32[]{:S(2)}) collective-permute-start(f32[3,4,64,64]{3,2,1,0:T(8,128)S(1)} %pad_maximum_fusion.2), channel_id=1, source_target_pairs={{0,8},{8,16},{16,24},{1,9},{9,17},{17,25},{2,10},{10,18},{18,26},{... | collective-permute-start | bytes 589832 | tf_op jit(solution)/shard_map/ppermute | solution.py:113
  94.7 0.4 fusion.54
  95.1 4.3 %collective-permute-done.5 = f32[3,4,64,64]{3,2,1,0:T(8,128)S(1)} collective-permute-done((f32[3,4,64,64]{3,2,1,0:T(8,128)S(1)}, f32[3,4,64,64]{3,2,1,0:T(8,128)S(1)}, u32[]{:S(2)}, u32[]{:S(2)}) %collective-permute-start.5) | collective-permute-done | bytes 196640 | tf_op jit(solution)/shard_map/ppermute | solution.py:113
  99.4 0.3 convolution_bitcast_fusion.1
  99.7 0.3 convolution_select_fusion.1
  100.1 0.3 convolution_bitcast_fusion.12
  100.4 0.3 fusion.10
  100.7 0.3 convolution_bitcast_fusion.10
  101.2 0.3 convolution_bitcast_fusion.11
  101.5 0.3 convolution_add_fusion.3
  101.8 0.3 fusion.65
  102.1 4.4 %collective-permute-start.6 = (f32[3,4,64,64]{3,2,1,0:T(8,128)S(1)}, f32[3,4,64,64]{3,2,1,0:T(8,128)S(1)}, u32[]{:S(2)}, u32[]{:S(2)}) collective-permute-start(f32[3,4,64,64]{3,2,1,0:T(8,128)S(1)} %pad_maximum_fusion.3), channel_id=1, source_target_pairs={{0,8},{8,16},{16,24},{1,9},{9,17},{17,25},{2,10},{10,18},{18,26},{... | collective-permute-start | bytes 589832 | tf_op jit(solution)/shard_map/ppermute | solution.py:113
  106.5 0.4 fusion.50
  106.9 4.3 %collective-permute-done.6 = f32[3,4,64,64]{3,2,1,0:T(8,128)S(1)} collective-permute-done((f32[3,4,64,64]{3,2,1,0:T(8,128)S(1)}, f32[3,4,64,64]{3,2,1,0:T(8,128)S(1)}, u32[]{:S(2)}, u32[]{:S(2)}) %collective-permute-start.6) | collective-permute-done | bytes 196640 | tf_op jit(solution)/shard_map/ppermute | solution.py:113
  111.2 0.3 convolution_bitcast_fusion
  111.5 0.3 convolution_select_fusion
  112.1 0.2 fusion.19
  113.2 0.9 add_bitcast_fusion
  114.1 0.5 fusion.20
  114.6 0.9 fusion.1
  (59 shorter events, 3.9 us)
Async XLA Ops:
  7.2 66.0 %all-gather.3.cloned.1.call-start = ((), (), s32[]{:S(2)}) async-start(), calls=%async_computation | async-start | bytes 3538944 | tf_op jit(solution)/shard_map/all_gather | solution.py:93
  7.2 4.9 %copy-start.2 = (f32[1,4,64,128]{3,2,1,0:T(8,128)S(1)}, f32[1,4,64,128]{3,2,1,0:T(8,128)}, u32[]{:S(2)}) copy-start(f32[1,4,64,128]{3,2,1,0:T(8,128)} %param.14) | copy-start | bytes 393220
  8.5 9.0 %copy-start.8 = (s32[4,2]{0,1:T(2,128)S(1)}, s32[4,2]{0,1:T(2,128)}, u32[]{:S(2)}) copy-start(s32[4,2]{0,1:T(2,128)} %param.17) | copy-start | bytes 100
  11.1 64.4 %copy-start.1 = (f32[3,4,64,64]{3,2,1,0:T(8,128)S(1)}, f32[3,4,64,64]{3,2,1,0:T(8,128)}, u32[]{:S(2)}) copy-start(f32[3,4,64,64]{3,2,1,0:T(8,128)} %param.15) | copy-start | bytes 589828
  11.1 64.4 %copy-start.7 = (f32[1,4]{1,0:T(1,128)S(1)}, f32[1,4]{1,0:T(1,128)}, u32[]{:S(2)}) copy-start(f32[1,4]{1,0:T(1,128)} %param.16) | copy-start | bytes 52
  11.2 64.4 %copy-start = (f32[64,64,1]{1,0,2:T(8,128)S(1)}, f32[64,64,1]{1,0,2:T(8,128)}, u32[]{:S(2)}) copy-start(f32[64,64,1]{1,0,2:T(8,128)} %constant.92) | copy-start | bytes 49156
  12.2 7.4 %collective-permute-start = (f32[4,64,3]{2,1,0:T(8,128)S(1)}, f32[4,64,3]{2,1,0:T(8,128)S(1)}, u32[]{:S(2)}, u32[]{:S(2)}) collective-permute-start(f32[4,64,3]{2,1,0:T(8,128)S(1)} %get-tuple-element.23), channel_id=1, source_target_pairs={{0,4},{1,5},{2,6},{3,7},{8,12},{9,13},{10,14},{11,15},{16,20},{17,... | collective-permute-start | bytes 9224 | tf_op jit(solution)/shard_map/ppermute | solution.py:47
  16.2 5.7 %collective-permute-start.1 = (f32[4,64,3]{2,1,0:T(8,128)S(1)}, f32[4,64,3]{2,1,0:T(8,128)S(1)}, u32[]{:S(2)}, u32[]{:S(2)}) collective-permute-start(f32[4,64,3]{2,1,0:T(8,128)S(1)} %get-tuple-element.24), channel_id=1, source_target_pairs={{4,0},{5,1},{6,2},{7,3},{12,8},{13,9},{14,10},{15,11},{20,16},{21,... | collective-permute-start | bytes 9224 | tf_op jit(solution)/shard_map/ppermute | solution.py:48
  22.0 61.3 %collective-permute-start.2 = (f32[4,3,134]{2,1,0:T(4,128)S(1)}, f32[4,3,134]{2,1,0:T(4,128)S(1)}, u32[]{:S(2)}, u32[]{:S(2)}) collective-permute-start(f32[4,3,134]{2,1,0:T(4,128)S(1)} %get-tuple-element.10), channel_id=1, source_target_pairs={{0,1},{1,2},{2,3},{4,5},{5,6},{6,7},{8,9},{9,10},{10,11},{12,13},{... | collective-permute-start | bytes 19304 | tf_op jit(solution)/shard_map/ppermute | solution.py:47
  25.2 58.1 %collective-permute-start.3 = (f32[4,3,134]{2,1,0:T(4,128)S(1)}, f32[4,3,134]{2,1,0:T(4,128)S(1)}, u32[]{:S(2)}, u32[]{:S(2)}) collective-permute-start(f32[4,3,134]{2,1,0:T(4,128)S(1)} %get-tuple-element.11), channel_id=1, source_target_pairs={{1,0},{2,1},{3,2},{5,4},{6,5},{7,6},{9,8},{10,9},{11,10},{13,12},{... | collective-permute-start | bytes 19304 | tf_op jit(solution)/shard_map/ppermute | solution.py:48
  73.2 3.8 %copy-start.3 = (f32[64,64,1]{1,0,2:T(8,128)S(1)}, f32[64,64,1]{1,0,2:T(8,128)}, u32[]{:S(2)}) copy-start(f32[64,64,1]{1,0,2:T(8,128)} %constant.93) | copy-start | bytes 49156
  75.5 12.1 %copy-start.4 = (f32[64,64]{1,0:T(8,128)S(1)}, f32[64,64]{1,0:T(8,128)}, u32[]{:S(2)}) copy-start(f32[64,64]{1,0:T(8,128)} %constant.86.clone) | copy-start | bytes 49156
  75.5 12.1 %copy-start.5 = (f32[64,64]{1,0:T(8,128)S(1)}, f32[64,64]{1,0:T(8,128)}, u32[]{:S(2)}) copy-start(f32[64,64]{1,0:T(8,128)} %constant.87.clone) | copy-start | bytes 49156
  77.5 10.1 %collective-permute-start.4 = (f32[3,4,64,64]{3,2,1,0:T(8,128)S(1)}, f32[3,4,64,64]{3,2,1,0:T(8,128)S(1)}, u32[]{:S(2)}, u32[]{:S(2)}) collective-permute-start(f32[3,4,64,64]{3,2,1,0:T(8,128)S(1)} %pad_maximum_fusion.1), channel_id=1, source_target_pairs={{0,8},{8,16},{16,24},{1,9},{9,17},{17,25},{2,10},{10,18},{18,26},{... | collective-permute-start | bytes 589832 | tf_op jit(solution)/shard_map/ppermute | solution.py:113
  90.3 9.1 %collective-permute-start.5 = (f32[3,4,64,64]{3,2,1,0:T(8,128)S(1)}, f32[3,4,64,64]{3,2,1,0:T(8,128)S(1)}, u32[]{:S(2)}, u32[]{:S(2)}) collective-permute-start(f32[3,4,64,64]{3,2,1,0:T(8,128)S(1)} %pad_maximum_fusion.2), channel_id=1, source_target_pairs={{0,8},{8,16},{16,24},{1,9},{9,17},{17,25},{2,10},{10,18},{18,26},{... | collective-permute-start | bytes 589832 | tf_op jit(solution)/shard_map/ppermute | solution.py:113
  102.1 9.1 %collective-permute-start.6 = (f32[3,4,64,64]{3,2,1,0:T(8,128)S(1)}, f32[3,4,64,64]{3,2,1,0:T(8,128)S(1)}, u32[]{:S(2)}, u32[]{:S(2)}) collective-permute-start(f32[3,4,64,64]{3,2,1,0:T(8,128)S(1)} %pad_maximum_fusion.3), channel_id=1, source_target_pairs={{0,8},{8,16},{16,24},{1,9},{9,17},{17,25},{2,10},{10,18},{18,26},{... | collective-permute-start | bytes 589832 | tf_op jit(solution)/shard_map/ppermute | solution.py:113
  106.9 7.2 %copy-start.6 = (f32[256,256]{1,0:T(8,128)S(1)}, f32[256,256]{1,0:T(8,128)}, u32[]{:S(2)}) copy-start(f32[256,256]{1,0:T(8,128)} %constant.85.clone) | copy-start | bytes 786436
Sparse Core Ops, SparseCore 0:
  12.2 60.9 all-gather.2
